TPU v7x, 512 devices: a whole 4x4x16 slice. The times are simulated.
512 devices in a mesh: section: 8 (over x, core), dp: 32 (over z, y_lo), mp: 2 (over y_hi).
Axes of the slice: x: 4, y: 4 (y_hi: 2, y_lo: 2; y = y_hi * 2 + y_lo), z: 16, core: 2. Of those that a mesh axis runs over, the one named last changes fastest.
Arguments:
- layer_inputs: bfloat16 [8, 128, 4096], P('section', None, 'mp'), may hold values from -6 to 6
- pre_act: bfloat16 [8, 128, 8192], P('section', None, 'dp'), may hold values from -6 to 6
- out_grad: bfloat16 [128, 4096], P(None, 'mp'), may hold values from -4 to 4
- w_in: bfloat16 [32, 8, 32, 4096], P('dp', 'section', None, 'mp'), may hold values from -0.09375 to 0.09375
- w_out: bfloat16 [32, 8, 32, 4096], P('dp', 'section', None, 'mp'), may hold values from -0.0625 to 0.0625
Outputs:
- in_grads: bfloat16 [8, 128, 4096], P('section', None, 'mp')
- grad_in: float32 [32, 8, 32, 4096], P('dp', 'section', None, 'mp')
- grad_out: float32 [32, 8, 32, 4096], P('dp', 'section', None, 'mp')
All inputs are finite; a program needn't handle non-finite values.
Results may differ from a plain program's by a relative error of at most 0.035.
Values may be sent and summed in bfloat16 or wider, within the bound.
No kernel may reach another device: no remote copies, remote signals or barrier semaphores. Data moves between devices by JAX's collectives and lax.ppermute only.
A program may use at most 64 MiB of HBM per device.

v0:
```python
import jax
import jax.numpy as jnp
from jax import lax
from jax.sharding import Mesh
from jax.sharding import PartitionSpec as P

MICRO = 2
DP = ("dp_0", "dp_1")


def sent_together(arrays, axis, dim, along):
    both = jnp.concatenate(arrays, axis=along)
    result, at, outs = (lax.all_gather(both, axis, axis=dim, tiled=True), 0, [])
    for a in arrays:
        outs.append(lax.slice_in_dim(result, at, at + a.shape[along], axis=along))
        at += a.shape[along]
    return tuple(outs)


def over_pieces(value, axis):
    return lax.all_gather(value, axis).astype(jnp.float32).sum(0)


def over_axes(value, axes):
    for axis in axes:
        value = lax.psum(value, axis)
    return value


def shifted(value, axis, by):
    size = lax.axis_size(axis)
    pairs = [(i, i + by) for i in range(size) if 0 <= i + by < size]
    return lax.ppermute(value, axis, pairs)


def in_one_piece(arrays, axis, dim, along):
    ends, at = ([], 0)
    for a in arrays[:-1]:
        at += a.shape[along]
        ends.append(at)
    both = jnp.concatenate(arrays, axis=along)
    return tuple(
        jnp.split(lax.psum_scatter(both, axis, scatter_dimension=dim, tiled=True), ends, axis=along)
    )


def gelu_slope(value):
    cdf = 0.5 * (1.0 + lax.erf(value * 0.7071067811865476))
    dens = jnp.exp(-0.5 * value * value) * 0.3989422804014327
    return cdf + value * dens


def by_tokens(left, right):
    return lax.dot_general(
        left, right, (((0,), (0,)), ((), ())), preferred_element_type=jnp.float32
    )


def body(layer_inputs, pre_act, out_grad, w_in, w_out):
    sections = lax.axis_size("section")
    spot = lax.axis_index("section")
    tok_rows = out_grad.shape[0]
    block = tok_rows // MICRO
    width = out_grad.shape[1]
    full_in, full_out = sent_together((w_in, w_out), "section", 1, 0)
    units = full_in.shape[1] * full_in.shape[2]
    per_block = full_in.shape[2]
    in_rows = full_in.reshape(units, width)
    out_rows = full_out.reshape(units, width)
    inputs = layer_inputs[0]
    saved = pre_act[0]
    is_last = spot == sections - 1

    def advance(step, state):
        incoming, dys, gees, results = state
        micro_id = step - (sections - 1 - spot)
        valid = jnp.logical_and(micro_id >= 0, micro_id < MICRO)
        begin = jnp.clip(micro_id, 0, MICRO - 1) * block
        given = lax.dynamic_slice_in_dim(out_grad, begin, block, 0)
        upper = jnp.where(is_last, given, incoming)
        partial_value = lax.dot_general(
            upper, out_rows, (((1,), (1,)), ((), ())), preferred_element_type=jnp.float32
        )
        summed = over_pieces(partial_value.astype(jnp.bfloat16), "mp").astype(jnp.float32)
        rows_pre = lax.dynamic_slice_in_dim(saved, begin, block, 0).astype(jnp.float32)
        gee = (summed * gelu_slope(rows_pre)).astype(jnp.bfloat16)
        branch = jnp.dot(gee, in_rows, preferred_element_type=jnp.float32)
        total = over_axes(branch.astype(jnp.bfloat16), DP).astype(jnp.float32)
        result = (upper.astype(jnp.float32) + total).astype(jnp.bfloat16)
        outgoing = shifted(result, "section", -1)
        old_dy = lax.dynamic_slice_in_dim(dys, begin, block, 0)
        old_gee = lax.dynamic_slice_in_dim(gees, begin, block, 0)
        old_res = lax.dynamic_slice_in_dim(results, begin, block, 0)
        dys = lax.dynamic_update_slice_in_dim(dys, jnp.where(valid, upper, old_dy), begin, 0)
        gees = lax.dynamic_update_slice_in_dim(gees, jnp.where(valid, gee, old_gee), begin, 0)
        results = lax.dynamic_update_slice_in_dim(
            results, jnp.where(valid, result, old_res), begin, 0
        )
        return (outgoing, dys, gees, results)

    start_state = (
        jnp.zeros((block, width), jnp.bfloat16),
        jnp.zeros((tok_rows, width), jnp.bfloat16),
        jnp.zeros((tok_rows, units), jnp.bfloat16),
        jnp.zeros((tok_rows, width), jnp.bfloat16),
    )
    final_state = lax.fori_loop(0, sections + MICRO - 1, advance, start_state)
    dys = final_state[1]
    gees = final_state[2]
    results = final_state[3]
    hidden = jax.nn.gelu(saved.astype(jnp.float32), approximate=False).astype(jnp.bfloat16)
    term_in = by_tokens(gees, inputs).reshape(1, sections, per_block, width)
    term_out = by_tokens(hidden, dys).reshape(1, sections, per_block, width)
    grad_in, grad_out = tuple(
        (
            part.astype(jnp.float32)
            for part in in_one_piece(
                (term_in.astype(jnp.bfloat16), term_out.astype(jnp.bfloat16)), "section", 1, 0
            )
        )
    )
    return (results[None], grad_in, grad_out)


def solution(mesh):
    split = Mesh(
        mesh.devices.reshape(mesh.shape["section"], 16, 2, mesh.shape["mp"]),
        ("section", "dp_0", "dp_1", "mp"),
    )
    placed = (
        P("section", None, "mp"),
        P("section", None, DP),
        P(None, "mp"),
        P(DP, "section", None, "mp"),
        P(DP, "section", None, "mp"),
    )
    return jax.shard_map(
        body,
        mesh=split,
        in_specs=placed,
        out_specs=(
            P("section", None, "mp"),
            P(DP, "section", None, "mp"),
            P(DP, "section", None, "mp"),
        ),
        check_vma=False,
    )
```

profile of v0, /device:TPU:8, one launch (start us, length us, event | category | flops | bytes accessed | tf_op | source)
XLA Modules:
  0.0 1952.7 jit_solution(7781573785871670471)
XLA Ops:
  10.9 37.2 %all-gather.5.cloned.1.call-done = bf16[2,8,32,2048]{3,2,1,0:T(8,128)(2,1)} async-done(((bf16[2,1,32,2048]{3,2,1,0:T(8,128)(2,1)}), bf16[2,8,32,2048]{3,2,1,0:T(8,128)(2,1)}) %all-gather.5.cloned.1.call-update) | async-done | bytes 2097168 | tf_op jit(solution)/shard_map/all_gather | solution.py:13
  52.0 1801.6 %while.21 = (s32[]{:T(128)}, bf16[64,2048]{1,0:T(8,128)(2,1)}, bf16[128,2048]{1,0:T(8,128)(2,1)S(1)}, bf16[128,256]{1,0:T(8,128)(2,1)}, bf16[128,2048]{1,0:T(8,1...) while((s32[]{:T(128)}, bf16[64,2048]{1,0:T(8,128)(2,1)}, ...), condition=%wide.region_4.5_spmd, body=%wide.region_0.4_spmd.sunk | while | flops 135970816 | bytes 11010468 | solution.py:107
  53.6 6.1 all-gather.2
  60.8 137.2 %all-reduce.7.cloned.1.call-done = bf16[64,2048]{1,0:T(8,128)(2,1)} async-done(((bf16[64,2048]{1,0:T(8,128)(2,1)}), bf16[64,2048]{1,0:T(8,128)(2,1)}) %all-reduce.7.cloned.1.call-update) | async-done | bytes 262160 | tf_op jit(solution)/shard_map/while/body/eval_jaxpr/psum | solution.py:26
  198.0 45.2 %all-reduce.9.cloned.1.call-done = bf16[64,2048]{1,0:T(8,128)(2,1)} async-done(((bf16[64,2048]{1,0:T(8,128)(2,1)}), bf16[64,2048]{1,0:T(8,128)(2,1)}) %all-reduce.9.cloned.1.call-update) | async-done | bytes 262160 | tf_op jit(solution)/shard_map/while/body/eval_jaxpr/psum | solution.py:26
  243.2 1.9 select_dynamic-update-slice_fusion.7
  251.1 6.1 all-gather.2
  258.3 140.3 %all-reduce.7.cloned.1.call-done = bf16[64,2048]{1,0:T(8,128)(2,1)} async-done(((bf16[64,2048]{1,0:T(8,128)(2,1)}), bf16[64,2048]{1,0:T(8,128)(2,1)}) %all-reduce.7.cloned.1.call-update) | async-done | bytes 262160 | tf_op jit(solution)/shard_map/while/body/eval_jaxpr/psum | solution.py:26
  398.6 45.1 %all-reduce.9.cloned.1.call-done = bf16[64,2048]{1,0:T(8,128)(2,1)} async-done(((bf16[64,2048]{1,0:T(8,128)(2,1)}), bf16[64,2048]{1,0:T(8,128)(2,1)}) %all-reduce.9.cloned.1.call-update) | async-done | bytes 262160 | tf_op jit(solution)/shard_map/while/body/eval_jaxpr/psum | solution.py:26
  451.5 6.1 all-gather.2
  458.7 140.3 %all-reduce.7.cloned.1.call-done = bf16[64,2048]{1,0:T(8,128)(2,1)} async-done(((bf16[64,2048]{1,0:T(8,128)(2,1)}), bf16[64,2048]{1,0:T(8,128)(2,1)}) %all-reduce.7.cloned.1.call-update) | async-done | bytes 262160 | tf_op jit(solution)/shard_map/while/body/eval_jaxpr/psum | solution.py:26
  599.0 45.2 %all-reduce.9.cloned.1.call-done = bf16[64,2048]{1,0:T(8,128)(2,1)} async-done(((bf16[64,2048]{1,0:T(8,128)(2,1)}), bf16[64,2048]{1,0:T(8,128)(2,1)}) %all-reduce.9.cloned.1.call-update) | async-done | bytes 262160 | tf_op jit(solution)/shard_map/while/body/eval_jaxpr/psum | solution.py:26
  652.1 6.1 all-gather.2
  659.3 140.3 %all-reduce.7.cloned.1.call-done = bf16[64,2048]{1,0:T(8,128)(2,1)} async-done(((bf16[64,2048]{1,0:T(8,128)(2,1)}), bf16[64,2048]{1,0:T(8,128)(2,1)}) %all-reduce.7.cloned.1.call-update) | async-done | bytes 262160 | tf_op jit(solution)/shard_map/while/body/eval_jaxpr/psum | solution.py:26
  799.6 45.2 %all-reduce.9.cloned.1.call-done = bf16[64,2048]{1,0:T(8,128)(2,1)} async-done(((bf16[64,2048]{1,0:T(8,128)(2,1)}), bf16[64,2048]{1,0:T(8,128)(2,1)}) %all-reduce.9.cloned.1.call-update) | async-done | bytes 262160 | tf_op jit(solution)/shard_map/while/body/eval_jaxpr/psum | solution.py:26
  852.7 6.1 all-gather.2
  859.9 140.3 %all-reduce.7.cloned.1.call-done = bf16[64,2048]{1,0:T(8,128)(2,1)} async-done(((bf16[64,2048]{1,0:T(8,128)(2,1)}), bf16[64,2048]{1,0:T(8,128)(2,1)}) %all-reduce.7.cloned.1.call-update) | async-done | bytes 262160 | tf_op jit(solution)/shard_map/while/body/eval_jaxpr/psum | solution.py:26
  1000.1 45.2 %all-reduce.9.cloned.1.call-done = bf16[64,2048]{1,0:T(8,128)(2,1)} async-done(((bf16[64,2048]{1,0:T(8,128)(2,1)}), bf16[64,2048]{1,0:T(8,128)(2,1)}) %all-reduce.9.cloned.1.call-update) | async-done | bytes 262160 | tf_op jit(solution)/shard_map/while/body/eval_jaxpr/psum | solution.py:26
  1053.3 6.1 all-gather.2
  1060.4 140.3 %all-reduce.7.cloned.1.call-done = bf16[64,2048]{1,0:T(8,128)(2,1)} async-done(((bf16[64,2048]{1,0:T(8,128)(2,1)}), bf16[64,2048]{1,0:T(8,128)(2,1)}) %all-reduce.7.cloned.1.call-update) | async-done | bytes 262160 | tf_op jit(solution)/shard_map/while/body/eval_jaxpr/psum | solution.py:26
  1200.7 45.2 %all-reduce.9.cloned.1.call-done = bf16[64,2048]{1,0:T(8,128)(2,1)} async-done(((bf16[64,2048]{1,0:T(8,128)(2,1)}), bf16[64,2048]{1,0:T(8,128)(2,1)}) %all-reduce.9.cloned.1.call-update) | async-done | bytes 262160 | tf_op jit(solution)/shard_map/while/body/eval_jaxpr/psum | solution.py:26
  1253.8 6.1 all-gather.2
  1261.0 140.3 %all-reduce.7.cloned.1.call-done = bf16[64,2048]{1,0:T(8,128)(2,1)} async-done(((bf16[64,2048]{1,0:T(8,128)(2,1)}), bf16[64,2048]{1,0:T(8,128)(2,1)}) %all-reduce.7.cloned.1.call-update) | async-done | bytes 262160 | tf_op jit(solution)/shard_map/while/body/eval_jaxpr/psum | solution.py:26
  1401.3 45.1 %all-reduce.9.cloned.1.call-done = bf16[64,2048]{1,0:T(8,128)(2,1)} async-done(((bf16[64,2048]{1,0:T(8,128)(2,1)}), bf16[64,2048]{1,0:T(8,128)(2,1)}) %all-reduce.9.cloned.1.call-update) | async-done | bytes 262160 | tf_op jit(solution)/shard_map/while/body/eval_jaxpr/psum | solution.py:26
  1454.2 6.1 all-gather.2
  1461.4 140.3 %all-reduce.7.cloned.1.call-done = bf16[64,2048]{1,0:T(8,128)(2,1)} async-done(((bf16[64,2048]{1,0:T(8,128)(2,1)}), bf16[64,2048]{1,0:T(8,128)(2,1)}) %all-reduce.7.cloned.1.call-update) | async-done | bytes 262160 | tf_op jit(solution)/shard_map/while/body/eval_jaxpr/psum | solution.py:26
  1601.7 45.1 %all-reduce.9.cloned.1.call-done = bf16[64,2048]{1,0:T(8,128)(2,1)} async-done(((bf16[64,2048]{1,0:T(8,128)(2,1)}), bf16[64,2048]{1,0:T(8,128)(2,1)}) %all-reduce.9.cloned.1.call-update) | async-done | bytes 262160 | tf_op jit(solution)/shard_map/while/body/eval_jaxpr/psum | solution.py:26
  1654.7 6.1 all-gather.2
  1661.8 140.3 %all-reduce.7.cloned.1.call-done = bf16[64,2048]{1,0:T(8,128)(2,1)} async-done(((bf16[64,2048]{1,0:T(8,128)(2,1)}), bf16[64,2048]{1,0:T(8,128)(2,1)}) %all-reduce.7.cloned.1.call-update) | async-done | bytes 262160 | tf_op jit(solution)/shard_map/while/body/eval_jaxpr/psum | solution.py:26
  1802.1 45.2 %all-reduce.9.cloned.1.call-done = bf16[64,2048]{1,0:T(8,128)(2,1)} async-done(((bf16[64,2048]{1,0:T(8,128)(2,1)}), bf16[64,2048]{1,0:T(8,128)(2,1)}) %all-reduce.9.cloned.1.call-update) | async-done | bytes 262160 | tf_op jit(solution)/shard_map/while/body/eval_jaxpr/psum | solution.py:26
  1859.1 84.4 %all-reduce.5.cloned.1.call-done = bf16[2,8,32,2048]{3,2,1,0:T(8,128)(2,1)} async-done(((bf16[2,8,32,2048]{3,2,1,0:T(8,128)(2,1)}), bf16[2,8,32,2048]{3,2,1,0:T(8,128)(2,1)}) %all-reduce.5.cloned.1.call-update) | async-done | bytes 2097168
  1943.5 2.4 dynamic-slice_convert_fusion
  (146 shorter events, 91.6 us)
Async XLA Ops:
  7.2 1848.7 %copy-start = (bf16[1,128,2048]{2,1,0:T(8,128)(2,1)S(1)}, bf16[1,128,2048]{2,1,0:T(8,128)(2,1)}, u32[]{:S(2)}) copy-start(bf16[1,128,2048]{2,1,0:T(8,128)(2,1)} %param.7) | copy-start | bytes 1572868
  7.2 40.9 %all-gather.5.cloned.1.call-start = ((), (), s32[]{:S(2)}) async-start(), calls=%async_computation | async-start | bytes 2359296 | tf_op jit(solution)/shard_map/all_gather | solution.py:13
  10.9 41.1 %copy-start.2 = (bf16[1,128,256]{2,1,0:T(8,128)(2,1)S(1)}, bf16[1,128,256]{2,1,0:T(8,128)(2,1)}, u32[]{:S(2)}) copy-start(bf16[1,128,256]{2,1,0:T(8,128)(2,1)} %param.8) | copy-start | bytes 196612
  52.0 146.0 %all-reduce.7.cloned.1.call-start = ((), (), s32[]{:S(2)}) async-start(), calls=%async_computation.2 | async-start | bytes 524288 | tf_op jit(solution)/shard_map/while/body/eval_jaxpr/psum | solution.py:26
  60.7 182.5 %all-reduce.9.cloned.1.call-start = ((), (), s32[]{:S(2)}) async-start(), calls=%async_computation.3 | async-start | bytes 524288 | tf_op jit(solution)/shard_map/while/body/eval_jaxpr/psum | solution.py:26
  245.2 3.6 collective-permute-start
  249.5 149.0 %all-reduce.7.cloned.1.call-start = ((), (), s32[]{:S(2)}) async-start(), calls=%async_computation.2 | async-start | bytes 524288 | tf_op jit(solution)/shard_map/while/body/eval_jaxpr/psum | solution.py:26
  258.3 185.4 %all-reduce.9.cloned.1.call-start = ((), (), s32[]{:S(2)}) async-start(), calls=%async_computation.3 | async-start | bytes 524288 | tf_op jit(solution)/shard_map/while/body/eval_jaxpr/psum | solution.py:26
  445.6 3.6 collective-permute-start
  449.2 0.7 copy-start.1
  449.9 149.0 %all-reduce.7.cloned.1.call-start = ((), (), s32[]{:S(2)}) async-start(), calls=%async_computation.2 | async-start | bytes 524288 | tf_op jit(solution)/shard_map/while/body/eval_jaxpr/psum | solution.py:26
  458.7 185.6 %all-reduce.9.cloned.1.call-start = ((), (), s32[]{:S(2)}) async-start(), calls=%async_computation.3 | async-start | bytes 524288 | tf_op jit(solution)/shard_map/while/body/eval_jaxpr/psum | solution.py:26
  646.2 3.6 collective-permute-start
  650.5 149.0 %all-reduce.7.cloned.1.call-start = ((), (), s32[]{:S(2)}) async-start(), calls=%async_computation.2 | async-start | bytes 524288 | tf_op jit(solution)/shard_map/while/body/eval_jaxpr/psum | solution.py:26
  659.2 185.6 %all-reduce.9.cloned.1.call-start = ((), (), s32[]{:S(2)}) async-start(), calls=%async_computation.3 | async-start | bytes 524288 | tf_op jit(solution)/shard_map/while/body/eval_jaxpr/psum | solution.py:26
  846.7 3.6 collective-permute-start
  851.1 149.0 %all-reduce.7.cloned.1.call-start = ((), (), s32[]{:S(2)}) async-start(), calls=%async_computation.2 | async-start | bytes 524288 | tf_op jit(solution)/shard_map/while/body/eval_jaxpr/psum | solution.py:26
  859.8 185.6 %all-reduce.9.cloned.1.call-start = ((), (), s32[]{:S(2)}) async-start(), calls=%async_computation.3 | async-start | bytes 524288 | tf_op jit(solution)/shard_map/while/body/eval_jaxpr/psum | solution.py:26
  1047.3 3.6 collective-permute-start
  1051.7 149.0 %all-reduce.7.cloned.1.call-start = ((), (), s32[]{:S(2)}) async-start(), calls=%async_computation.2 | async-start | bytes 524288 | tf_op jit(solution)/shard_map/while/body/eval_jaxpr/psum | solution.py:26
  1060.4 185.6 %all-reduce.9.cloned.1.call-start = ((), (), s32[]{:S(2)}) async-start(), calls=%async_computation.3 | async-start | bytes 524288 | tf_op jit(solution)/shard_map/while/body/eval_jaxpr/psum | solution.py:26
  1247.9 3.6 collective-permute-start
  1252.2 149.0 %all-reduce.7.cloned.1.call-start = ((), (), s32[]{:S(2)}) async-start(), calls=%async_computation.2 | async-start | bytes 524288 | tf_op jit(solution)/shard_map/while/body/eval_jaxpr/psum | solution.py:26
  1261.0 185.4 %all-reduce.9.cloned.1.call-start = ((), (), s32[]{:S(2)}) async-start(), calls=%async_computation.3 | async-start | bytes 524288 | tf_op jit(solution)/shard_map/while/body/eval_jaxpr/psum | solution.py:26
  1448.3 3.6 collective-permute-start
  1452.6 149.0 %all-reduce.7.cloned.1.call-start = ((), (), s32[]{:S(2)}) async-start(), calls=%async_computation.2 | async-start | bytes 524288 | tf_op jit(solution)/shard_map/while/body/eval_jaxpr/psum | solution.py:26
  1461.4 185.4 %all-reduce.9.cloned.1.call-start = ((), (), s32[]{:S(2)}) async-start(), calls=%async_computation.3 | async-start | bytes 524288 | tf_op jit(solution)/shard_map/while/body/eval_jaxpr/psum | solution.py:26
  1648.7 3.6 collective-permute-start
  1653.1 149.0 %all-reduce.7.cloned.1.call-start = ((), (), s32[]{:S(2)}) async-start(), calls=%async_computation.2 | async-start | bytes 524288 | tf_op jit(solution)/shard_map/while/body/eval_jaxpr/psum | solution.py:26
  1661.8 185.6 %all-reduce.9.cloned.1.call-start = ((), (), s32[]{:S(2)}) async-start(), calls=%async_computation.3 | async-start | bytes 524288 | tf_op jit(solution)/shard_map/while/body/eval_jaxpr/psum | solution.py:26
  1849.3 3.6 collective-permute-start
  1853.6 89.8 %all-reduce.5.cloned.1.call-start = ((), (), s32[]{:S(2)}) async-start(), calls=%async_computation.1 | async-start | bytes 4194304
  (8 other events, 5.6 us)
Sparse Core Ops, SparseCore 0:
  10.7 37.3 all-gather.4
  60.9 137.0 all-reduce.6
  200.9 42.3 all-reduce.8
  258.4 140.1 all-reduce.6
  401.3 42.3 all-reduce.8
  458.8 140.1 all-reduce.6
  601.8 42.3 all-reduce.8
  659.4 140.1 all-reduce.6
  802.4 42.3 all-reduce.8
  859.9 140.1 all-reduce.6
  1003.0 42.3 all-reduce.8
  1060.5 140.1 all-reduce.6
  1203.6 42.3 all-reduce.8
  1261.1 140.1 all-reduce.6
  1404.0 42.3 all-reduce.8
  1461.5 140.1 all-reduce.6
  1604.4 42.3 all-reduce.8
  1661.9 140.1 all-reduce.6
  1805.0 42.3 all-reduce.8
  1857.9 85.4 all-reduce.4
where the time goes:
time: 1950 us
  waiting for transfers between devices  1800 us (92%)
  blocking collectives  54.8 us (3%)
  other arithmetic  47.1 us (2%)
    psum x18, waiting for transfers between devices, over_axes(): value = lax.psum(value, axis)  1670 us
    unnamed x3, waiting for transfers between devices  84.4 us
    all_gather x9, blocking collectives, over_pieces(): return lax.all_gather(value, axis).astype(jnp.float32).sum(0)  54.8 us
  transfers between devices with their start and end apart: 29, of which 29 were waited for; matrix products, arithmetic and copies ran while one was open for 1% of the time, Pallas kernels for 0%

commit v1 on v0

--- a/solution.py
+++ b/solution.py
@@ -23,7 +23,7 @@
 
 def over_axes(value, axes):
     for axis in axes:
-        value = lax.psum(value, axis)
+        value = jnp.sum(lax.all_gather(value, axis), axis=0)
     return value
 
 

time: 1950 us -> 1080 us (0.55)
  waiting for transfers between devices: 1800 us -> 818 us
  blocking collectives: 54.8 us -> 120 us
  other arithmetic: 47.1 us -> 93.7 us
    psum x18 -> x0, waiting for transfers between devices: 1670 us -> none  [over_axes(): value = lax.psum(value, axis)]
    all_gather x0 -> x9, waiting for transfers between devices: none -> 694 us  [over_axes(): value = jnp.sum(lax.all_gather(value, axis), axis=0)]
    all_gather x0 -> x9, blocking collectives: none -> 65.2 us  [over_axes(): value = jnp.sum(lax.all_gather(value, axis), axis=0)]
    reduce_sum x0 -> x18, other arithmetic: none -> 41.2 us  [over_axes(): value = jnp.sum(lax.all_gather(value, axis), axis=0)]
  transfers between devices with their start and end apart: 29 -> 20, of which waited for: 29 -> 20; matrix products, arithmetic and copies ran while one was open for 1% -> 1% of each run, Pallas kernels for 0% -> 0%
where the time goes in v1:
time: 1080 us
  waiting for transfers between devices  818 us (76%)
  blocking collectives  120 us (11%)
  other arithmetic  93.7 us (9%)
  matrix products  15 us (1%)
  between operations  13.8 us (1%)
  starting transfers between devices  11.6 us (1%)
    all_gather x9, waiting for transfers between devices, over_axes(): value = jnp.sum(lax.all_gather(value, axis), axis=0)  694 us
    unnamed x3, waiting for transfers between devices  79.9 us
    all_gather x9, blocking collectives, over_axes(): value = jnp.sum(lax.all_gather(value, axis), axis=0)  65.2 us
    all_gather x9, blocking collectives, over_pieces(): return lax.all_gather(value, axis).astype(jnp.float32).sum(0)  54.8 us
    reduce_sum x18, other arithmetic, over_axes(): value = jnp.sum(lax.all_gather(value, axis), axis=0)  41.2 us
    all_gather x1, waiting for transfers between devices, sent_together(): result, at, outs = (lax.all_gather(both, axis, axis=dim, tiled=True), 0, [])  37.2 us
  transfers between devices with their start and end apart: 20, of which 20 were waited for; matrix products, arithmetic and copies ran while one was open for 1% of the time, Pallas kernels for 0%

profile of v1, /device:TPU:8, one launch (start us, length us, event | category | flops | bytes accessed | tf_op | source)
XLA Modules:
  0.0 1079.3 jit_solution(6154446689883070917)
XLA Ops:
  10.9 37.2 %all-gather.12.cloned.1.call-done = bf16[2,8,32,2048]{3,2,1,0:T(8,128)(2,1)} async-done(((bf16[2,1,32,2048]{3,2,1,0:T(8,128)(2,1)}), bf16[2,8,32,2048]{3,2,1,0:T(8,128)(2,1)}) %all-gather.12.cloned.1.call-update) | async-done | bytes 2097168 | tf_op jit(solution)/shard_map/all_gather | solution.py:13
  52.1 932.6 %while.22 = (s32[]{:T(128)}, bf16[64,2048]{1,0:T(8,128)(2,1)S(1)}, bf16[128,2048]{1,0:T(8,128)(2,1)}, bf16[128,256]{1,0:T(8,128)(2,1)}, bf16[128,2048]{1,0:T(8,1...) while((s32[]{:T(128)}, bf16[64,2048]{1,0:T(8,128)(2,1)S(1)}, ...), condition=%wide.region_4.5_spmd, body=%wide.region_0.4_spmd.sunk | while | flops 137805824 | bytes 26215272 | solution.py:107
  54.4 6.1 all-gather.6
  61.5 78.5 %all-gather.14.cloned.1.call-done = bf16[1024,2048]{1,0:T(8,128)(2,1)} async-done(((bf16[64,2048]{1,0:T(8,128)(2,1)}), bf16[1024,2048]{1,0:T(8,128)(2,1)}) %all-gather.14.cloned.1.call-update) | async-done | bytes 4194320 | tf_op jit(solution)/shard_map/while/body/eval_jaxpr/all_gather | solution.py:26
  140.1 3.7 reduce_sum.50
  143.8 7.2 all-gather.8
  159.4 6.1 all-gather.6
  166.6 76.9 %all-gather.14.cloned.1.call-done = bf16[1024,2048]{1,0:T(8,128)(2,1)} async-done(((bf16[64,2048]{1,0:T(8,128)(2,1)}), bf16[1024,2048]{1,0:T(8,128)(2,1)}) %all-gather.14.cloned.1.call-update) | async-done | bytes 4194320 | tf_op jit(solution)/shard_map/while/body/eval_jaxpr/all_gather | solution.py:26
  243.5 3.7 reduce_sum.50
  247.2 7.2 all-gather.8
  262.9 6.1 all-gather.6
  270.0 76.9 %all-gather.14.cloned.1.call-done = bf16[1024,2048]{1,0:T(8,128)(2,1)} async-done(((bf16[64,2048]{1,0:T(8,128)(2,1)}), bf16[1024,2048]{1,0:T(8,128)(2,1)}) %all-gather.14.cloned.1.call-update) | async-done | bytes 4194320 | tf_op jit(solution)/shard_map/while/body/eval_jaxpr/all_gather | solution.py:26
  350.7 7.2 all-gather.8
  366.3 6.1 all-gather.6
  373.4 76.9 %all-gather.14.cloned.1.call-done = bf16[1024,2048]{1,0:T(8,128)(2,1)} async-done(((bf16[64,2048]{1,0:T(8,128)(2,1)}), bf16[1024,2048]{1,0:T(8,128)(2,1)}) %all-gather.14.cloned.1.call-update) | async-done | bytes 4194320 | tf_op jit(solution)/shard_map/while/body/eval_jaxpr/all_gather | solution.py:26
  454.1 7.2 all-gather.8
  469.7 6.1 all-gather.6
  476.9 77.0 %all-gather.14.cloned.1.call-done = bf16[1024,2048]{1,0:T(8,128)(2,1)} async-done(((bf16[64,2048]{1,0:T(8,128)(2,1)}), bf16[1024,2048]{1,0:T(8,128)(2,1)}) %all-gather.14.cloned.1.call-update) | async-done | bytes 4194320 | tf_op jit(solution)/shard_map/while/body/eval_jaxpr/all_gather | solution.py:26
  557.6 7.2 all-gather.8
  573.2 6.1 all-gather.6
  580.3 77.0 %all-gather.14.cloned.1.call-done = bf16[1024,2048]{1,0:T(8,128)(2,1)} async-done(((bf16[64,2048]{1,0:T(8,128)(2,1)}), bf16[1024,2048]{1,0:T(8,128)(2,1)}) %all-gather.14.cloned.1.call-update) | async-done | bytes 4194320 | tf_op jit(solution)/shard_map/while/body/eval_jaxpr/all_gather | solution.py:26
  661.0 7.2 all-gather.8
  676.7 6.1 all-gather.6
  683.8 77.0 %all-gather.14.cloned.1.call-done = bf16[1024,2048]{1,0:T(8,128)(2,1)} async-done(((bf16[64,2048]{1,0:T(8,128)(2,1)}), bf16[1024,2048]{1,0:T(8,128)(2,1)}) %all-gather.14.cloned.1.call-update) | async-done | bytes 4194320 | tf_op jit(solution)/shard_map/while/body/eval_jaxpr/all_gather | solution.py:26
  764.5 7.2 all-gather.8
  780.1 6.1 all-gather.6
  787.2 77.0 %all-gather.14.cloned.1.call-done = bf16[1024,2048]{1,0:T(8,128)(2,1)} async-done(((bf16[64,2048]{1,0:T(8,128)(2,1)}), bf16[1024,2048]{1,0:T(8,128)(2,1)}) %all-gather.14.cloned.1.call-update) | async-done | bytes 4194320 | tf_op jit(solution)/shard_map/while/body/eval_jaxpr/all_gather | solution.py:26
  867.9 7.2 all-gather.8
  883.6 6.1 all-gather.6
  890.7 76.9 %all-gather.14.cloned.1.call-done = bf16[1024,2048]{1,0:T(8,128)(2,1)} async-done(((bf16[64,2048]{1,0:T(8,128)(2,1)}), bf16[1024,2048]{1,0:T(8,128)(2,1)}) %all-gather.14.cloned.1.call-update) | async-done | bytes 4194320 | tf_op jit(solution)/shard_map/while/body/eval_jaxpr/all_gather | solution.py:26
  971.4 7.2 all-gather.8
  990.5 79.9 %all-reduce.3.cloned.1.call-done = bf16[2,8,32,2048]{3,2,1,0:T(8,128)(2,1)} async-done(((bf16[2,8,32,2048]{3,2,1,0:T(8,128)(2,1)}), bf16[2,8,32,2048]{3,2,1,0:T(8,128)(2,1)}) %all-reduce.3.cloned.1.call-update) | async-done | bytes 2097168
  (128 shorter events, 126.7 us)
Async XLA Ops:
  7.2 980.1 %copy-start = (bf16[1,128,2048]{2,1,0:T(8,128)(2,1)S(1)}, bf16[1,128,2048]{2,1,0:T(8,128)(2,1)}, u32[]{:S(2)}) copy-start(bf16[1,128,2048]{2,1,0:T(8,128)(2,1)} %param.7) | copy-start | bytes 1572868
  7.2 40.9 %all-gather.12.cloned.1.call-start = ((), (), s32[]{:S(2)}) async-start(), calls=%async_computation | async-start | bytes 2359296 | tf_op jit(solution)/shard_map/all_gather | solution.py:13
  10.9 41.2 %copy-start.1 = (bf16[1,128,256]{2,1,0:T(8,128)(2,1)S(1)}, bf16[1,128,256]{2,1,0:T(8,128)(2,1)}, u32[]{:S(2)}) copy-start(bf16[1,128,256]{2,1,0:T(8,128)(2,1)} %param.8) | copy-start | bytes 196612
  52.1 88.0 %all-gather.14.cloned.1.call-start = ((), (), s32[]{:S(2)}) async-start(), calls=%async_computation.2 | async-start | bytes 4456448 | tf_op jit(solution)/shard_map/while/body/eval_jaxpr/all_gather | solution.py:26
  153.7 3.4 collective-permute-start
  157.1 86.4 %all-gather.14.cloned.1.call-start = ((), (), s32[]{:S(2)}) async-start(), calls=%async_computation.2 | async-start | bytes 4456448 | tf_op jit(solution)/shard_map/while/body/eval_jaxpr/all_gather | solution.py:26
  257.2 3.4 collective-permute-start
  260.6 86.4 %all-gather.14.cloned.1.call-start = ((), (), s32[]{:S(2)}) async-start(), calls=%async_computation.2 | async-start | bytes 4456448 | tf_op jit(solution)/shard_map/while/body/eval_jaxpr/all_gather | solution.py:26
  360.6 3.4 collective-permute-start
  364.0 86.4 %all-gather.14.cloned.1.call-start = ((), (), s32[]{:S(2)}) async-start(), calls=%async_computation.2 | async-start | bytes 4456448 | tf_op jit(solution)/shard_map/while/body/eval_jaxpr/all_gather | solution.py:26
  464.0 3.4 collective-permute-start
  467.4 86.4 %all-gather.14.cloned.1.call-start = ((), (), s32[]{:S(2)}) async-start(), calls=%async_computation.2 | async-start | bytes 4456448 | tf_op jit(solution)/shard_map/while/body/eval_jaxpr/all_gather | solution.py:26
  567.5 3.4 collective-permute-start
  570.9 86.4 %all-gather.14.cloned.1.call-start = ((), (), s32[]{:S(2)}) async-start(), calls=%async_computation.2 | async-start | bytes 4456448 | tf_op jit(solution)/shard_map/while/body/eval_jaxpr/all_gather | solution.py:26
  671.0 3.4 collective-permute-start
  674.4 86.4 %all-gather.14.cloned.1.call-start = ((), (), s32[]{:S(2)}) async-start(), calls=%async_computation.2 | async-start | bytes 4456448 | tf_op jit(solution)/shard_map/while/body/eval_jaxpr/all_gather | solution.py:26
  774.4 3.4 collective-permute-start
  777.8 86.4 %all-gather.14.cloned.1.call-start = ((), (), s32[]{:S(2)}) async-start(), calls=%async_computation.2 | async-start | bytes 4456448 | tf_op jit(solution)/shard_map/while/body/eval_jaxpr/all_gather | solution.py:26
  877.9 3.4 collective-permute-start
  881.3 86.4 %all-gather.14.cloned.1.call-start = ((), (), s32[]{:S(2)}) async-start(), calls=%async_computation.2 | async-start | bytes 4456448 | tf_op jit(solution)/shard_map/while/body/eval_jaxpr/all_gather | solution.py:26
  981.3 3.4 collective-permute-start
  984.8 85.6 %all-reduce.3.cloned.1.call-start = ((), (), s32[]{:S(2)}) async-start(), calls=%async_computation.1 | async-start | bytes 4194304
Sparse Core Ops, SparseCore 0:
  10.7 37.3 all-gather.11
  61.6 78.3 all-gather.13
  166.7 76.7 all-gather.13
  270.1 76.7 all-gather.13
  373.6 76.7 all-gather.13
  477.0 76.8 all-gather.13
  580.4 76.7 all-gather.13
  683.9 76.7 all-gather.13
  787.4 76.7 all-gather.13
  890.9 76.7 all-gather.13
  989.3 81.0 all-reduce.2
